TPU v7x, 32 devices: a whole 2x2x4 slice. The times are simulated.
32 devices in a mesh: section: 4 (over y, x), stem: 8 (over z, core).
Axes of the slice: x: 2, y: 2, z: 4, core: 2. Of those that a mesh axis runs over, the one named last changes fastest.
Arguments:
- bitstrings: int32 [4, 4, 32, 3], P('section'), may hold values 0 or 1
- boundary: float32 [2, 2048], replicated, may hold values from -6 to 6
- stem_tensor: float32 [4, 2, 2048, 8, 2048], P('section', None, 'stem'), may hold values from -0.09375 to 0.09375
- probe_vectors: float32 [4, 2, 2048], P('section'), may hold values from -0.09375 to 0.09375
- inbound_permutations: int32 [4, 2048], replicated, may hold values from 0 to 2047, each once within a row
Outputs:
- amplitudes: float32 [4, 2, 4, 32], P('section')
Inputs may be any that keep to these rules, and one draw needn't show every extreme that they name: `inbound_permutations`: each row of relabeling names every number of 0 to 2047 once.
All inputs are finite; a program needn't handle non-finite values. No bound on the sum of `bitstrings` on one device may be relied on, other than what follows from the above.
Results may differ from a plain program's by a relative error of at most 0.0003.
Values sent between devices are 32-bit elements; how exact they have to be, the bound alone decides.
A program may use at most 128 MiB of HBM per device.

v0:
```python
import jax
import jax.numpy as jnp
from jax import lax
from jax.sharding import PartitionSpec as P

HIGH = lax.Precision.HIGH
HIGHEST = lax.Precision.HIGHEST


def halves(x):
    hi = lax.reduce_precision(x, 8, 7)
    return (hi.astype(jnp.bfloat16), (x - hi).astype(jnp.bfloat16))


def select_columns(x, chosen):
    rows = x.shape[0]
    pick = (jnp.arange(x.shape[1], dtype=jnp.int32)[:, None] == chosen[None, :]).astype(
        jnp.bfloat16
    )
    hi, lo = halves(x)
    both = jnp.dot(jnp.concatenate([hi, lo]), pick, preferred_element_type=jnp.float32)
    return both[:rows] + both[rows:]


def local(bitstrings, boundary, stem_tensor, probe_vectors, inbound_permutations):
    section = lax.axis_index("section")
    sections = lax.axis_size("section")
    rank = lax.axis_index("stem")
    rows, settings, width = stem_tensor.shape[2:]
    bonds = boundary.shape[1]
    micro, batch, qubits = bitstrings.shape[1:]
    count = micro * batch
    powers = jnp.left_shift(jnp.int32(1), jnp.arange(qubits, dtype=jnp.int32))
    own_setting = jnp.sum(bitstrings[0] * powers, axis=-1).reshape(count)
    setting = lax.all_gather(own_setting, "section")
    probe = probe_vectors[0]
    perm = inbound_permutations

    def flat(plane):
        return stem_tensor[0, plane].reshape(rows * settings, width)

    def own_rows(row):
        return lax.dynamic_slice_in_dim(row, rank * rows, rows)

    zeros_a = jnp.zeros((2 * settings, bonds), jnp.float32)

    def first_forward():
        t_re, t_im = (stem_tensor[0, 0], stem_tensor[0, 1])
        b = jnp.dot(
            boundary,
            (jnp.arange(bonds, dtype=jnp.int32)[:, None] == own_rows(perm[0])[None, :]).astype(
                jnp.float32
            ),
            precision=HIGHEST,
        )
        b_re, b_im = (b[0][:, None, None], b[1][:, None, None])
        u_re = jnp.sum(b_re * t_re - b_im * t_im, axis=0)
        u_im = jnp.sum(b_re * t_im + b_im * t_re, axis=0)
        return jnp.concatenate([u_re, u_im])

    def last_backward():
        t_re, t_im = (stem_tensor[0, 0], stem_tensor[0, 1])
        v_re = jnp.sum(t_re * probe[0] - t_im * probe[1], axis=-1)
        v_im = jnp.sum(t_re * probe[1] + t_im * probe[0], axis=-1)
        v = jnp.concatenate([v_re.T, v_im.T])
        return lax.dynamic_update_slice_in_dim(zeros_a, v, rank * rows, 1)

    idle = lambda: zeros_a
    vectors = lax.switch(section, [first_forward, idle, idle, last_backward])

    def product_with_probe(v_re, v_im):
        return (
            jnp.dot(v_re, probe[0], precision=HIGHEST) - jnp.dot(v_im, probe[1], precision=HIGHEST),
            jnp.dot(v_re, probe[1], precision=HIGHEST) + jnp.dot(v_im, probe[0], precision=HIGHEST),
        )

    amp_first = jnp.stack(product_with_probe(vectors[:settings], vectors[settings:]))
    moved = lax.ppermute(vectors, "section", [(0, 1), (3, 2)])
    vectors = lax.psum(moved, "stem")
    ends = settings + 1
    pairs = settings * settings
    zeros_u = jnp.zeros((2 * pairs, bonds), jnp.float32)
    zeros_w = jnp.zeros((rows, settings * 2 * ends), jnp.float32)
    zeros_p = jnp.zeros((2, pairs), jnp.float32)

    def second_forward():
        x = select_columns(vectors, own_rows(perm[1])).reshape(2, settings, 1, rows, 1)
        same = jnp.eye(settings, dtype=jnp.float32).reshape(1, 1, settings, 1, settings)
        spread = (x * same).reshape(2 * pairs, rows * settings)
        p_re = jnp.dot(spread, flat(0), precision=HIGH)
        p_im = jnp.dot(spread, flat(1), precision=HIGH)
        u_re = p_re[:pairs] - p_im[pairs:]
        u_im = p_im[:pairs] + p_re[pairs:]
        amp = jnp.stack(product_with_probe(u_re, u_im))
        u = select_columns(jnp.concatenate([u_re, u_im]), perm[2])
        return (u, zeros_w, amp)

    def second_backward():
        place = (perm[3][:, None] == jnp.arange(bonds, dtype=jnp.int32)[None, :]).astype(
            jnp.bfloat16
        )
        hi, lo = halves(vectors)
        both = jnp.dot(jnp.concatenate([hi, lo]), place, preferred_element_type=jnp.float32)
        v = (both[: 2 * settings] + both[2 * settings :]).reshape(2, settings, bonds)
        v = jnp.concatenate([v, probe[:, None, :]], axis=1).reshape(2 * ends, bonds)
        q_re = lax.dot_general(flat(0), v, (((1,), (1,)), ((), ())), precision=HIGH)
        q_im = lax.dot_general(flat(1), v, (((1,), (1,)), ((), ())), precision=HIGH)
        w_re = q_re[:, :ends] - q_im[:, ends:]
        w_im = q_re[:, ends:] + q_im[:, :ends]
        w = jnp.concatenate([w_re, w_im], axis=1).reshape(rows, settings * 2 * ends)
        return (zeros_u, w, zeros_p)

    none = lambda: (zeros_u, zeros_w, zeros_p)
    u, w, amp_second = lax.switch(section, [none, second_forward, second_backward, none])
    w = lax.ppermute(w, "section", [(2, 1)])
    w = lax.all_gather(w, "stem", axis=0, tiled=True)
    joined = jnp.dot(u, w, precision=HIGH).reshape(2, pairs, settings, 2, ends)
    j_re = (joined[0, :, :, 0] - joined[1, :, :, 1]).reshape(pairs, settings * ends)
    j_im = (joined[0, :, :, 1] + joined[1, :, :, 0]).reshape(pairs, settings * ends)
    onehot = lambda ids, size: (ids[:, None] == jnp.arange(size, dtype=jnp.int32)[None, :]).astype(
        jnp.float32
    )
    front = onehot(setting[0] * settings + setting[1], pairs)
    first = jnp.dot(amp_first, onehot(setting[0], settings).T, precision=HIGHEST)
    first = jnp.where(section == 0, first, 0.0)
    second = jnp.dot(amp_second, front.T, precision=HIGHEST)
    third_pick = onehot(setting[2] * ends + settings, settings * ends)
    fourth_pick = onehot(setting[2] * ends + setting[3], settings * ends)
    rows_re = jnp.dot(front, j_re, precision=HIGHEST)
    rows_im = jnp.dot(front, j_im, precision=HIGHEST)
    third = jnp.stack(
        [jnp.sum(rows_re * third_pick, axis=1), jnp.sum(rows_im * third_pick, axis=1)]
    )
    fourth = jnp.stack(
        [jnp.sum(rows_re * fourth_pick, axis=1), jnp.sum(rows_im * fourth_pick, axis=1)]
    )
    partial = jnp.stack([first, second, third, fourth])
    total = lax.psum(partial, ("section", "stem"))
    own = lax.dynamic_index_in_dim(total, section, 0, False)
    return own.reshape(1, 2, micro, batch)


def solution(mesh):
    return jax.shard_map(
        local,
        mesh=mesh,
        in_specs=(
            P("section", None, None, None),
            P(),
            P("section", None, "stem", None, None),
            P("section", None, None),
            P(),
        ),
        out_specs=P("section", None, None, None),
        check_vma=False,
    )
```

profile of v0, /device:TPU:0, one launch (start us, length us, event | category | flops | bytes accessed | tf_op | source)
XLA Modules:
  0.0 223.1 jit_solution(2156276009823240268)
XLA Ops:
  6.5 0.0 all-reduce.2.cloned.1.call-start
  6.5 15.1 %conditional.2 = (f32[16,2048]{1,0:T(8,128)}, f32[8,2048]{1,0:T(8,128)S(1)}, f32[8,2048]{1,0:T(8,128)S(1)}) conditional(s32[]{:T(128)} %clamp.4, (s32[4,2048]{1,0:T(4,128)}, s32[]{:T(128)}, f32[2,2048]{1,0:T(2,128)}, f32[1,2,256,8,2048]{4,3,2,1,0:T(8,128)}) %tuple.41, () %tuple.42, () %tuple.43, ...), branch_computations={%region_0.3_spmd, %region_3.4_spmd, %region_4.0_spmd, %region_5.8_... | conditional | flops 46661636 | bytes 34078796 | solution.py:69
  6.5 0.8 slice.108
  7.3 1.4 fusion.5
  8.8 12.2 %fusion.1 = (f32[8,2048]{1,0:T(8,128)S(1)}, f32[8,2048]{1,0:T(8,128)S(1)}) fusion(f32[1,2,256,8,2048]{4,3,2,1,0:T(8,128)} %get-tuple-element.43, f32[256]{0:T(256)S(1)} %bitcast.210, f32[256]{0:T(256)S(1)} %bitcast.209), kind=kLoop, calls=%fused_computation.3 | loop fusion | flops 33521664 | bytes 33687552 | tf_op jit(solution)/shard_map/cond/branch_0_fun/reduce_sum | solution.py:57
  21.0 0.6 pad_maximum_fusion
  21.6 1.3 collective-permute-start
  22.9 4.0 %collective-permute-done = f32[16,2048]{1,0:T(8,128)S(1)} collective-permute-done((f32[16,2048]{1,0:T(8,128)}, f32[16,2048]{1,0:T(8,128)S(1)}, u32[]{:S(2)}, u32[]{:S(2)}) %collective-permute-start) | collective-permute-done | bytes 131104 | tf_op jit(solution)/shard_map/ppermute | solution.py:78
  26.9 0.0 copy-start.3
  26.9 0.6 copy-done.3
  27.5 0.0 all-reduce.2.cloned.1.call-update
  27.6 0.0 all-gather.3.cloned.1.call-start
  27.6 58.5 %all-reduce.2.cloned.1.call-done = f32[16,2048]{1,0:T(8,128)} async-done(((f32[16,2048]{1,0:T(8,128)}), f32[16,2048]{1,0:T(8,128)}) %all-reduce.2.cloned.1.call-update) | async-done | bytes 131088 | tf_op jit(solution)/shard_map/psum | solution.py:79
  86.1 0.0 copy-start.4
  86.1 0.0 copy-start
  86.1 0.4 conditional.3
  86.1 0.1 broadcast_in_dim.32
  86.5 0.7 collective-permute-start.1
  87.1 0.0 collective-permute-done.1
  87.2 0.0 copy-start.2
  87.2 0.7 copy-done.2
  87.9 0.0 all-gather.3.cloned.1.call-update
  87.9 0.0 copy-done.4
  87.9 0.1 fusion.80
  88.0 0.1 reshape.101
  88.1 63.0 %all-gather = s32[4,1,128]{2,1,0:T(1,128)S(1)} all-gather(s32[1,1,128]{2,1,0:T(1,128)S(1)} %reshape.101), channel_id=1, replica_groups=mesh['section'=4,'stem'=8] {'section'}, dimensions={0}, use_global_device_ids=true | all-gather | bytes 2560 | tf_op jit(solution)/shard_map/all_gather | solution.py:35
  151.1 0.9 convolution_bitcast_fusion.7
  152.1 0.0 copy-done
  152.1 0.3 convolution_bitcast_fusion.5
  152.3 0.3 fusion.67
  152.6 0.3 fusion.69
  152.9 0.2 fusion.65
  153.1 0.3 convolution_bitcast_fusion.4
  153.4 17.8 %all-gather.3.cloned.1.call-done = f32[2048,144]{1,0:T(8,128)} async-done(((f32[256,144]{1,0:T(8,128)}), f32[2048,144]{1,0:T(8,128)}) %all-gather.3.cloned.1.call-update) | async-done | bytes 1179664 | tf_op jit(solution)/shard_map/all_gather | solution.py:116
  171.1 3.4 %fusion.95 = f32[128,144]{0,1:T(8,128)S(1)} fusion(f32[128,2048]{1,0:T(8,128)S(1)} %get-tuple-element.66, f32[2048,144]{1,0:T(8,128)} %all-gather.3.cloned.1.call-done), kind=kOutput, calls=%fused_computation.158 | convolution fusion | flops 226492416 | bytes 2301952 | tf_op jit(solution)/shard_map/dot_general | solution.py:117
  174.5 0.1 reshape.99
  174.7 0.1 slice_subtract_fusion.2
  174.7 0.3 fusion.71
  175.0 0.3 select_reduce_fusion.2
  175.4 40.2 %psum.15 = f32[4,2,128]{2,1,0:T(2,128)S(1)} all-reduce(f32[4,2,128]{2,1,0:T(2,128)S(1)} %pad_maximum_fusion.5), channel_id=1, replica_groups=mesh['section'=4,'stem'=8] {'section','stem'}, use_global_device_ids=true, to_apply=%region_18.19 | all-reduce | flops 1024 | bytes 8192 | tf_op jit(solution)/shard_map/psum | solution.py:138
  215.5 0.7 reshape.100
  (10 shorter events, 0.1 us)
Async XLA Ops:
  6.5 79.5 %all-reduce.2.cloned.1.call-start = ((), (), s32[]{:S(2)}) async-start(), calls=%async_computation | async-start | bytes 262144 | tf_op jit(solution)/shard_map/psum | solution.py:79
  21.6 5.3 %collective-permute-start = (f32[16,2048]{1,0:T(8,128)}, f32[16,2048]{1,0:T(8,128)S(1)}, u32[]{:S(2)}, u32[]{:S(2)}) collective-permute-start(f32[16,2048]{1,0:T(8,128)} %get-tuple-element.64), channel_id=1, source_target_pairs={{0,8},{24,16},{1,9},{25,17},{2,10},{26,18},{3,11},{27,19},{4,12},{... | collective-permute-start | bytes 393224 | tf_op jit(solution)/shard_map/ppermute | solution.py:78
  26.9 0.6 copy-start.3
  27.6 143.6 %all-gather.3.cloned.1.call-start = ((), (), s32[]{:S(2)}) async-start(), calls=%async_computation.1 | async-start | bytes 2359296 | tf_op jit(solution)/shard_map/all_gather | solution.py:116
  86.1 1.9 copy-start.4
  86.1 66.0 %copy-start = (f32[1,2,2048]{2,1,0:T(2,128)S(1)}, f32[1,2,2048]{2,1,0:T(2,128)}, u32[]{:S(2)}) copy-start(f32[1,2,2048]{2,1,0:T(2,128)} %param.16) | copy-start | bytes 49156
  86.5 0.7 collective-permute-start.1
  87.2 0.7 copy-start.2
Sparse Core Ops, SparseCore 0:
  27.7 58.3 all-reduce.1
  88.0 83.0 all-gather.2
where the time goes:
time: 224 us; the launch traced here: 223 us
  blocking collectives  103 us (46%)
  waiting for transfers between devices  80.3 us (36%)
  between operations  13.5 us (6%)
  other arithmetic  13.1 us (6%)
  matrix products  7.6 us (3%)
  local copies, waits for them, and re-layouts  3.15 us (1%)
    all_gather x1, blocking collectives, local(): setting = lax.all_gather(own_setting, 'section')  63 us
    psum x1, waiting for transfers between devices, local(): vectors = lax.psum(moved, 'stem')  58.5 us
    psum x1, blocking collectives, local(): total = lax.psum(partial, ('section', 'stem'))  40.2 us
    all_gather x1, waiting for transfers between devices, local(): w = lax.all_gather(w, 'stem', axis=0, tiled=True)  17.8 us
    reduce_sum x1, other arithmetic, first_forward(): u_re = jnp.sum(b_re * t_re - b_im * t_im, axis=0)  12.2 us
  transfers between devices with their start and end apart: 4, of which 3 were waited for; matrix products, arithmetic and copies ran while one was open for 1% of the time, Pallas kernels for 0%

commit v1 on v0

--- a/solution.py
+++ b/solution.py
@@ -135,7 +135,7 @@
         [jnp.sum(rows_re * fourth_pick, axis=1), jnp.sum(rows_im * fourth_pick, axis=1)]
     )
     partial = jnp.stack([first, second, third, fourth])
-    total = lax.psum(partial, ("section", "stem"))
+    total = jnp.sum(lax.all_gather(partial, ("section", "stem")), axis=0)
     own = lax.dynamic_index_in_dim(total, section, 0, False)
     return own.reshape(1, 2, micro, batch)
 

time: 224 us -> 224 us (level)
    all_gather x0 -> x1, blocking collectives: none -> 40.5 us  [local(): total = jnp.sum(lax.all_gather(partial, ('section', 'stem')), axis=0)]
    psum x1 -> x0, blocking collectives: 40.2 us -> none  [local(): total = lax.psum(partial, ('section', 'stem'))]
where the time goes in v1:
time: 224 us; the launch traced here: 223 us
  blocking collectives  103 us (46%)
  waiting for transfers between devices  80.3 us (36%)
  between operations  13.5 us (6%)
  other arithmetic  13.1 us (6%)
  matrix products  7.6 us (3%)
  local copies, waits for them, and re-layouts  3.15 us (1%)
    all_gather x1, blocking collectives, local(): setting = lax.all_gather(own_setting, 'section')  63 us
    psum x1, waiting for transfers between devices, local(): vectors = lax.psum(moved, 'stem')  58.5 us
    all_gather x1, blocking collectives, local(): total = jnp.sum(lax.all_gather(partial, ('section', 'stem')), axis=0)  40.5 us
    all_gather x1, waiting for transfers between devices, local(): w = lax.all_gather(w, 'stem', axis=0, tiled=True)  17.8 us
    reduce_sum x1, other arithmetic, first_forward(): u_re = jnp.sum(b_re * t_re - b_im * t_im, axis=0)  12.2 us
  transfers between devices with their start and end apart: 4, of which 3 were waited for; matrix products, arithmetic and copies ran while one was open for 1% of the time, Pallas kernels for 0%

profile of v1, /device:TPU:0, one launch (start us, length us, event | category | flops | bytes accessed | tf_op | source)
XLA Modules:
  0.0 223.4 jit_solution(9189706416662337775)
XLA Ops:
  6.5 0.0 all-reduce.2.cloned.1.call-start
  6.5 15.1 %conditional.2 = (f32[16,2048]{1,0:T(8,128)}, f32[8,2048]{1,0:T(8,128)S(1)}, f32[8,2048]{1,0:T(8,128)S(1)}) conditional(s32[]{:T(128)} %clamp.4, (s32[4,2048]{1,0:T(4,128)}, s32[]{:T(128)}, f32[2,2048]{1,0:T(2,128)}, f32[1,2,256,8,2048]{4,3,2,1,0:T(8,128)}) %tuple.41, () %tuple.42, () %tuple.43, ...), branch_computations={%region_0.3_spmd, %region_3.4_spmd, %region_4.0_spmd, %region_5.8_... | conditional | flops 46661636 | bytes 34078796 | solution.py:69
  6.5 0.8 slice.108
  7.3 1.4 fusion.5
  8.8 12.2 %fusion.1 = (f32[8,2048]{1,0:T(8,128)S(1)}, f32[8,2048]{1,0:T(8,128)S(1)}) fusion(f32[1,2,256,8,2048]{4,3,2,1,0:T(8,128)} %get-tuple-element.43, f32[256]{0:T(256)S(1)} %bitcast.212, f32[256]{0:T(256)S(1)} %bitcast.211), kind=kLoop, calls=%fused_computation.3 | loop fusion | flops 33521664 | bytes 33687552 | tf_op jit(solution)/shard_map/cond/branch_0_fun/reduce_sum | solution.py:57
  21.0 0.6 pad_maximum_fusion
  21.6 1.3 collective-permute-start
  22.9 4.0 %collective-permute-done = f32[16,2048]{1,0:T(8,128)S(1)} collective-permute-done((f32[16,2048]{1,0:T(8,128)}, f32[16,2048]{1,0:T(8,128)S(1)}, u32[]{:S(2)}, u32[]{:S(2)}) %collective-permute-start) | collective-permute-done | bytes 131104 | tf_op jit(solution)/shard_map/ppermute | solution.py:78
  26.9 0.0 copy-start.3
  26.9 0.6 copy-done.3
  27.5 0.0 all-reduce.2.cloned.1.call-update
  27.6 0.0 all-gather.4.cloned.1.call-start
  27.6 58.5 %all-reduce.2.cloned.1.call-done = f32[16,2048]{1,0:T(8,128)} async-done(((f32[16,2048]{1,0:T(8,128)}), f32[16,2048]{1,0:T(8,128)}) %all-reduce.2.cloned.1.call-update) | async-done | bytes 131088 | tf_op jit(solution)/shard_map/psum | solution.py:79
  86.1 0.0 copy-start.4
  86.1 0.0 copy-start
  86.1 0.4 conditional.3
  86.1 0.1 broadcast_in_dim.32
  86.5 0.7 collective-permute-start.1
  87.1 0.0 collective-permute-done.1
  87.2 0.0 copy-start.2
  87.2 0.7 copy-done.2
  87.9 0.0 all-gather.4.cloned.1.call-update
  87.9 0.0 copy-done.4
  87.9 0.1 fusion.80
  88.0 0.1 reshape.102
  88.1 63.0 %all-gather.1 = s32[4,1,128]{2,1,0:T(1,128)S(1)} all-gather(s32[1,1,128]{2,1,0:T(1,128)S(1)} %reshape.102), channel_id=1, replica_groups=mesh['section'=4,'stem'=8] {'section'}, dimensions={0}, use_global_device_ids=true | all-gather | bytes 2560 | tf_op jit(solution)/shard_map/all_gather | solution.py:35
  151.1 0.9 convolution_bitcast_fusion.7
  152.1 0.0 copy-done
  152.1 0.3 convolution_bitcast_fusion.5
  152.3 0.3 fusion.67
  152.6 0.3 fusion.69
  152.9 0.2 fusion.65
  153.1 0.3 convolution_bitcast_fusion.4
  153.4 17.8 %all-gather.4.cloned.1.call-done = f32[2048,144]{1,0:T(8,128)} async-done(((f32[256,144]{1,0:T(8,128)}), f32[2048,144]{1,0:T(8,128)}) %all-gather.4.cloned.1.call-update) | async-done | bytes 1179664 | tf_op jit(solution)/shard_map/all_gather | solution.py:116
  171.1 3.4 %fusion.95 = f32[128,144]{0,1:T(8,128)S(1)} fusion(f32[128,2048]{1,0:T(8,128)S(1)} %get-tuple-element.66, f32[2048,144]{1,0:T(8,128)} %all-gather.4.cloned.1.call-done), kind=kOutput, calls=%fused_computation.158 | convolution fusion | flops 226492416 | bytes 2301952 | tf_op jit(solution)/shard_map/dot_general | solution.py:117
  174.5 0.1 reshape.99
  174.7 0.1 slice_subtract_fusion.2
  174.7 0.3 fusion.71
  175.0 0.3 select_reduce_fusion.2
  175.4 40.5 %all-gather = f32[128,2,128]{2,1,0:T(2,128)S(1)} all-gather(f32[4,2,128]{2,1,0:T(2,128)S(1)} %pad_maximum_fusion.5), channel_id=2, replica_groups=mesh['section'=4,'stem'=8] {'section','stem'}, dimensions={0}, use_global_device_ids=true | all-gather | bytes 135168 | tf_op jit(solution)/shard_map/all_gather | solution.py:138
  215.8 0.1 reduce_sum.95
  215.9 0.7 reshape.100
  (10 shorter events, 0.1 us)
Async XLA Ops:
  6.5 79.5 %all-reduce.2.cloned.1.call-start = ((), (), s32[]{:S(2)}) async-start(), calls=%async_computation | async-start | bytes 262144 | tf_op jit(solution)/shard_map/psum | solution.py:79
  21.6 5.3 %collective-permute-start = (f32[16,2048]{1,0:T(8,128)}, f32[16,2048]{1,0:T(8,128)S(1)}, u32[]{:S(2)}, u32[]{:S(2)}) collective-permute-start(f32[16,2048]{1,0:T(8,128)} %get-tuple-element.64), channel_id=1, source_target_pairs={{0,8},{24,16},{1,9},{25,17},{2,10},{26,18},{3,11},{27,19},{4,12},{... | collective-permute-start | bytes 393224 | tf_op jit(solution)/shard_map/ppermute | solution.py:78
  26.9 0.6 copy-start.3
  27.6 143.6 %all-gather.4.cloned.1.call-start = ((), (), s32[]{:S(2)}) async-start(), calls=%async_computation.1 | async-start | bytes 2359296 | tf_op jit(solution)/shard_map/all_gather | solution.py:116
  86.1 1.9 copy-start.4
  86.1 66.0 %copy-start = (f32[1,2,2048]{2,1,0:T(2,128)S(1)}, f32[1,2,2048]{2,1,0:T(2,128)}, u32[]{:S(2)}) copy-start(f32[1,2,2048]{2,1,0:T(2,128)} %param.16) | copy-start | bytes 49156
  86.5 0.7 collective-permute-start.1
  87.2 0.7 copy-start.2
Sparse Core Ops, SparseCore 0:
  27.7 58.3 all-reduce.1
  88.0 83.0 all-gather.3

commit v2 on v0

--- a/solution.py
+++ b/solution.py
@@ -135,7 +135,7 @@
         [jnp.sum(rows_re * fourth_pick, axis=1), jnp.sum(rows_im * fourth_pick, axis=1)]
     )
     partial = jnp.stack([first, second, third, fourth])
-    total = lax.psum(partial, ("section", "stem"))
+    total = lax.psum(lax.psum(partial, "stem"), "section")
     own = lax.dynamic_index_in_dim(total, section, 0, False)
     return own.reshape(1, 2, micro, batch)
 

time: 224 us -> 208 us (0.929)
  blocking collectives: 103 us -> 88.1 us
    psum x1 -> x2, blocking collectives: 40.2 us -> 25.1 us  [local(): total = lax.psum(lax.psum(partial, 'stem'), 'section')]
where the time goes in v2:
time: 208 us
  blocking collectives  88.1 us (42%)
  waiting for transfers between devices  80.2 us (39%)
  between operations  13.5 us (6%)
  other arithmetic  13.1 us (6%)
  matrix products  7.6 us (4%)
  local copies, waits for them, and re-layouts  3.15 us (2%)
    all_gather x1, blocking collectives, local(): setting = lax.all_gather(own_setting, 'section')  63 us
    psum x1, waiting for transfers between devices, local(): vectors = lax.psum(moved, 'stem')  58.4 us
    psum x2, blocking collectives, local(): total = lax.psum(lax.psum(partial, 'stem'), 'section')  25.1 us
    all_gather x1, waiting for transfers between devices, local(): w = lax.all_gather(w, 'stem', axis=0, tiled=True)  17.8 us
    reduce_sum x1, other arithmetic, first_forward(): u_re = jnp.sum(b_re * t_re - b_im * t_im, axis=0)  12.2 us
  transfers between devices with their start and end apart: 4, of which 3 were waited for; matrix products, arithmetic and copies ran while one was open for 1% of the time, Pallas kernels for 0%

profile of v2, /device:TPU:0, one launch (start us, length us, event | category | flops | bytes accessed | tf_op | source)
XLA Modules:
  0.0 208.0 jit_solution(15354438021009770072)
XLA Ops:
  6.5 0.0 all-reduce.2.cloned.1.call-start
  6.5 15.1 %conditional.2 = (f32[16,2048]{1,0:T(8,128)}, f32[8,2048]{1,0:T(8,128)S(1)}, f32[8,2048]{1,0:T(8,128)S(1)}) conditional(s32[]{:T(128)} %clamp.4, (s32[4,2048]{1,0:T(4,128)}, s32[]{:T(128)}, f32[2,2048]{1,0:T(2,128)}, f32[1,2,256,8,2048]{4,3,2,1,0:T(8,128)}) %tuple.41, () %tuple.42, () %tuple.43, ...), branch_computations={%region_0.3_spmd, %region_3.4_spmd, %region_4.0_spmd, %region_5.8_... | conditional | flops 46661636 | bytes 34078796 | solution.py:69
  6.5 0.8 slice.108
  7.3 1.4 fusion.5
  8.8 12.2 %fusion.1 = (f32[8,2048]{1,0:T(8,128)S(1)}, f32[8,2048]{1,0:T(8,128)S(1)}) fusion(f32[1,2,256,8,2048]{4,3,2,1,0:T(8,128)} %get-tuple-element.43, f32[256]{0:T(256)S(1)} %bitcast.210, f32[256]{0:T(256)S(1)} %bitcast.209), kind=kLoop, calls=%fused_computation.3 | loop fusion | flops 33521664 | bytes 33687552 | tf_op jit(solution)/shard_map/cond/branch_0_fun/reduce_sum | solution.py:57
  21.0 0.6 pad_maximum_fusion
  21.6 1.3 collective-permute-start
  22.9 4.0 %collective-permute-done = f32[16,2048]{1,0:T(8,128)S(1)} collective-permute-done((f32[16,2048]{1,0:T(8,128)}, f32[16,2048]{1,0:T(8,128)S(1)}, u32[]{:S(2)}, u32[]{:S(2)}) %collective-permute-start) | collective-permute-done | bytes 131104 | tf_op jit(solution)/shard_map/ppermute | solution.py:78
  26.9 0.0 copy-start.3
  26.9 0.6 copy-done.3
  27.5 0.0 all-reduce.2.cloned.1.call-update
  27.6 0.0 all-gather.3.cloned.1.call-start
  27.6 58.4 %all-reduce.2.cloned.1.call-done = f32[16,2048]{1,0:T(8,128)} async-done(((f32[16,2048]{1,0:T(8,128)}), f32[16,2048]{1,0:T(8,128)}) %all-reduce.2.cloned.1.call-update) | async-done | bytes 131088 | tf_op jit(solution)/shard_map/psum | solution.py:79
  86.1 0.0 copy-start.4
  86.1 0.0 copy-start
  86.1 0.4 conditional.3
  86.1 0.1 broadcast_in_dim.32
  86.4 0.7 collective-permute-start.1
  87.1 0.0 collective-permute-done.1
  87.1 0.0 copy-start.2
  87.1 0.7 copy-done.2
  87.9 0.0 all-gather.3.cloned.1.call-update
  87.9 0.0 copy-done.4
  87.9 0.1 fusion.80
  88.0 0.1 reshape.101
  88.1 63.0 %all-gather = s32[4,1,128]{2,1,0:T(1,128)S(1)} all-gather(s32[1,1,128]{2,1,0:T(1,128)S(1)} %reshape.101), channel_id=1, replica_groups=mesh['section'=4,'stem'=8] {'section'}, dimensions={0}, use_global_device_ids=true | all-gather | bytes 2560 | tf_op jit(solution)/shard_map/all_gather | solution.py:35
  151.1 0.9 convolution_bitcast_fusion.7
  152.0 0.0 copy-done
  152.0 0.3 convolution_bitcast_fusion.5
  152.3 0.3 fusion.67
  152.5 0.3 fusion.69
  152.8 0.2 fusion.65
  153.0 0.3 convolution_bitcast_fusion.4
  153.3 17.8 %all-gather.3.cloned.1.call-done = f32[2048,144]{1,0:T(8,128)} async-done(((f32[256,144]{1,0:T(8,128)}), f32[2048,144]{1,0:T(8,128)}) %all-gather.3.cloned.1.call-update) | async-done | bytes 1179664 | tf_op jit(solution)/shard_map/all_gather | solution.py:116
  171.1 3.4 %fusion.95 = f32[128,144]{0,1:T(8,128)S(1)} fusion(f32[128,2048]{1,0:T(8,128)S(1)} %get-tuple-element.66, f32[2048,144]{1,0:T(8,128)} %all-gather.3.cloned.1.call-done), kind=kOutput, calls=%fused_computation.158 | convolution fusion | flops 226492416 | bytes 2301952 | tf_op jit(solution)/shard_map/dot_general | solution.py:117
  174.5 0.1 reshape.99
  174.6 0.1 slice_subtract_fusion.2
  174.7 0.3 fusion.71
  175.0 0.3 select_reduce_fusion.2
  175.3 15.3 %psum.22 = f32[4,2,128]{2,1,0:T(2,128)S(1)} all-reduce(f32[4,2,128]{2,1,0:T(2,128)S(1)} %pad_maximum_fusion.5), channel_id=1, replica_groups=mesh['section'=4,'stem'=8] {'stem'}, use_global_device_ids=true, to_apply=%region_18.19 | all-reduce | flops 1024 | bytes 8192 | tf_op jit(solution)/shard_map/psum | solution.py:138
  190.6 9.8 %psum.23 = f32[4,2,128]{2,1,0:T(2,128)S(1)} all-reduce(f32[4,2,128]{2,1,0:T(2,128)S(1)} %psum.22), channel_id=1, replica_groups=mesh['section'=4,'stem'=8] {'section'}, use_global_device_ids=true, to_apply=%region_19.20 | all-reduce | flops 1024 | bytes 8192 | tf_op jit(solution)/shard_map/psum | solution.py:138
  200.4 0.7 reshape.100
  (10 shorter events, 0.1 us)
Async XLA Ops:
  6.5 79.5 %all-reduce.2.cloned.1.call-start = ((), (), s32[]{:S(2)}) async-start(), calls=%async_computation | async-start | bytes 262144 | tf_op jit(solution)/shard_map/psum | solution.py:79
  21.6 5.3 %collective-permute-start = (f32[16,2048]{1,0:T(8,128)}, f32[16,2048]{1,0:T(8,128)S(1)}, u32[]{:S(2)}, u32[]{:S(2)}) collective-permute-start(f32[16,2048]{1,0:T(8,128)} %get-tuple-element.64), channel_id=1, source_target_pairs={{0,8},{24,16},{1,9},{25,17},{2,10},{26,18},{3,11},{27,19},{4,12},{... | collective-permute-start | bytes 393224 | tf_op jit(solution)/shard_map/ppermute | solution.py:78
  26.9 0.6 copy-start.3
  27.6 143.5 %all-gather.3.cloned.1.call-start = ((), (), s32[]{:S(2)}) async-start(), calls=%async_computation.1 | async-start | bytes 2359296 | tf_op jit(solution)/shard_map/all_gather | solution.py:116
  86.1 1.8 copy-start.4
  86.1 66.0 %copy-start = (f32[1,2,2048]{2,1,0:T(2,128)S(1)}, f32[1,2,2048]{2,1,0:T(2,128)}, u32[]{:S(2)}) copy-start(f32[1,2,2048]{2,1,0:T(2,128)} %param.16) | copy-start | bytes 49156
  86.4 0.7 collective-permute-start.1
  87.1 0.7 copy-start.2
Sparse Core Ops, SparseCore 0:
  27.7 58.3 all-reduce.1
  88.0 83.0 all-gather.2
